TPU v7x, 32 devices: a whole 2x2x4 slice. The times are simulated.
32 devices in a mesh: row: 8 (over y, x, core), col: 4 (over z).
Axes of the slice: x: 2, y: 2, z: 4, core: 2. Of those that a mesh axis runs over, the one named last changes fastest.
Arguments:
- vectors: bfloat16 [32, 1024, 512], P('col', 'row'), may hold values from -6 to 6
- right_factors: bfloat16 [32, 32, 1024, 128], P('row', 'col'), may hold values from -0.1875 to 0.1875
- left_factors: bfloat16 [32, 32, 1024, 128], P('row', 'col'), may hold values from -0.125 to 0.125
- tile_ranks: int32 [32, 32], P('row', 'col'), may hold values from 16 to 128
- owner_map: int32 [32], replicated, may hold values from 0 to 31, as said below
Outputs:
- applied: bfloat16 [32, 1024, 512], P('row', 'col')
Inputs may be any that keep to these rules, and one draw needn't show every extreme that they name: owner_map is a permutation of 0 to 31; the 4 stored tile rows held by index i of row (stored rows i * 4 to i * 4 + 3) belong to 4 different indices of row of applied, i + c mod 8 for the same 4 offsets c at every i.
All inputs are finite; a program needn't handle non-finite values.
Results may differ from a plain program's by a relative error of at most 0.0066.
Values may be sent and summed in bfloat16 or wider, within the bound.
A program may use at most 128 MiB of HBM per device.

v0:
```python
import jax
import jax.numpy as jnp
from jax import lax
from jax.sharding import PartitionSpec as P


def masked_coeffs(products, tile_ranks, rank_width):
    columns = jnp.arange(rank_width, dtype=jnp.int32)
    kept_mask = columns[None, None, :] < tile_ranks[:, :, None]
    return jnp.where(kept_mask[:, :, :, None], products, 0.0).astype(jnp.bfloat16)


def build_buffer(payload, owner_map, cycle_size):
    held_rows = payload.shape[0]
    own_rows = lax.dynamic_slice_in_dim(owner_map, lax.axis_index("row") * held_rows, held_rows)
    target = own_rows // held_rows
    devices = jnp.arange(cycle_size, dtype=jnp.int32)
    matches = target[None, :] == devices[:, None]
    present = jnp.any(matches, axis=1)
    source_slot = jnp.sum(
        jnp.where(matches, jnp.arange(held_rows, dtype=jnp.int32)[None, :], 0), axis=1
    )
    picked = jnp.take(payload, source_slot, axis=0)
    return jnp.where(present[:, None, None], picked, jnp.zeros_like(picked))


def pick_rows(received, owner_map, held_rows):
    wanted = lax.axis_index("row") * held_rows + jnp.arange(held_rows, dtype=jnp.int32)
    matches = owner_map[None, :] == wanted[:, None]
    anchor = jnp.sum(
        jnp.where(matches, jnp.arange(owner_map.shape[0], dtype=jnp.int32)[None, :], 0), axis=1
    )
    return jnp.take(received, anchor // held_rows, axis=0)


def on_device(vectors, right_factors, left_factors, tile_ranks, owner_map):
    held_rows = right_factors.shape[0]
    rank_width = right_factors.shape[3]
    cycle_size = lax.axis_size("row")
    products = jnp.einsum(
        "ikbr,kbv->ikrv",
        right_factors,
        lax.all_gather(vectors, "row", axis=1, tiled=True),
        preferred_element_type=jnp.float32,
    )
    coeffs = masked_coeffs(products, tile_ranks, rank_width)
    partial_rows = jnp.einsum(
        "ikbr,ikrv->ibv", left_factors, coeffs, preferred_element_type=jnp.float32
    )
    summed = lax.psum_scatter(partial_rows, "col", scatter_dimension=1, tiled=True).astype(
        jnp.bfloat16
    )
    buffer = build_buffer(summed, owner_map, cycle_size)
    received = lax.all_to_all(buffer, "row", split_axis=0, concat_axis=0, tiled=True)
    applied = pick_rows(received, owner_map, held_rows)
    return applied


def solution(mesh):
    placed = (
        P("col", "row", None),
        P("row", "col", None, None),
        P("row", "col", None, None),
        P("row", "col"),
        P(),
    )
    return jax.shard_map(
        on_device, mesh=mesh, in_specs=placed, out_specs=P("row", "col", None), check_vma=False
    )
```

profile of v0, /device:TPU:0, one launch (start us, length us, event | category | flops | bytes accessed | tf_op | source)
XLA Modules:
  0.0 271.4 jit_solution(948302696471374495)
XLA Ops:
  6.5 0.0 all-gather.2.cloned.1.call-start
  6.5 0.7 all-gather.2.cloned.1.call-update
  7.3 0.0 reduce-scatter.2.cloned.1.call-start
  7.3 0.8 iota_compare_fusion
  8.1 58.2 %all-gather.2.cloned.1.call-done = bf16[8,1024,512]{2,1,0:T(8,128)(2,1)} async-done(((bf16[8,128,512]{2,1,0:T(8,128)(2,1)}), bf16[8,1024,512]{2,1,0:T(8,128)(2,1)}) %all-gather.2.cloned.1.call-update) | async-done | bytes 8388624 | tf_op jit(solution)/shard_map/all_gather | solution.py:43
  66.3 17.0 %fusion.7 = f32[4,1024,512]{1,2,0:T(8,128)} fusion(bf16[4,8,1024,128]{3,2,1,0:T(8,128)(2,1)} %param.7, pred[4,8,128]{2,1,0:T(8,128)(4,1)S(1)} %iota_compare_fusion, bf16[4,8,1024,128]{3,2,1,0:T(8,128)(2,1)} %param.6, bf16[8,1024,512]{2,1,0:T(8,128)(2,1)} %all-gather.2.cloned.1.call-done), kind=kOutput, calls=%fused_computation.9 | convolution fusion | flops 8594128896 | bytes 33558528 | tf_op jit(solution)/shard_map/ikbr,ikrv->ibv/dot_general | solution.py:47
  83.3 0.0 copy-start
  83.3 0.0 reduce-scatter.2.cloned.1.call-update
  83.3 0.6 copy-done
  83.9 0.1 and_select_fusion.1
  84.0 0.1 select_reduce_fusion
  84.1 0.1 fusion.14
  84.2 143.9 %reduce-scatter.2.cloned.1.call-done = f32[4,256,512]{1,2,0:T(8,128)} async-done(((f32[4,1024,512]{1,2,0:T(8,128)}), f32[4,256,512]{1,2,0:T(8,128)}) %reduce-scatter.2.cloned.1.call-update) | async-done | bytes 2097168 | tf_op jit(solution)/shard_map/reduce_scatter | solution.py:50
  228.1 1.7 convert_element_type.7
  229.8 0.7 gather_fusion
  230.5 1.6 select_select_fusion
  232.1 3.7 %all-to-all-start = ((bf16[8,256,512]{1,2,0:T(8,128)(2,1)}), bf16[8,256,512]{1,2,0:T(8,128)(2,1)S(1)}, u32[]{:S(2)}, u32[]{:S(2)}) async-start(bf16[8,256,512]{1,2,0:T(8,128)(2,1)} %select_select_fusion), calls=%async_computation.1 | async-start | bytes 4194304 | tf_op jit(solution)/shard_map/all_to_all | solution.py:54
  235.8 0.2 select_reduce_fusion.1
  236.0 26.4 %all-to-all-done = bf16[8,256,512]{1,2,0:T(8,128)(2,1)S(1)} async-done(((bf16[8,256,512]{1,2,0:T(8,128)(2,1)}), bf16[8,256,512]{1,2,0:T(8,128)(2,1)S(1)}, u32[]{:S(2)}, u32[]{:S(2)}) %all-to-all-start) | async-done | bytes 2097184 | tf_op jit(solution)/shard_map/all_to_all | solution.py:54
  262.4 0.6 gather_fusion.1
  263.0 0.2 broadcast_select_fusion
  263.2 1.3 copy.7
  (7 shorter events, 0.1 us)
Async XLA Ops:
  6.5 59.7 %all-gather.2.cloned.1.call-start = ((), (), s32[]{:S(2)}) async-start(), calls=%async_computation.2 | async-start | bytes 9437184 | tf_op jit(solution)/shard_map/all_gather | solution.py:43
  7.3 220.8 %reduce-scatter.2.cloned.1.call-start = ((), (), s32[]{:S(2)}) async-start(), calls=%async_computation.3 | async-start | bytes 10485760 | tf_op jit(solution)/shard_map/reduce_scatter | solution.py:50
  83.3 0.7 copy-start
  232.1 30.3 %all-to-all-start = ((bf16[8,256,512]{1,2,0:T(8,128)(2,1)}), bf16[8,256,512]{1,2,0:T(8,128)(2,1)S(1)}, u32[]{:S(2)}, u32[]{:S(2)}) async-start(bf16[8,256,512]{1,2,0:T(8,128)(2,1)} %select_select_fusion), calls=%async_computation.1 | async-start | bytes 4194304 | tf_op jit(solution)/shard_map/all_to_all | solution.py:54
Sparse Core Ops, SparseCore 0:
  9.2 56.9 all-gather.1
  83.4 144.6 reduce-scatter.1
where the time goes:
time: 272 us; the launch traced here: 271 us
  waiting for transfers between devices  229 us (84%)
  matrix products  17 us (6%)
  between operations  13.4 us (5%)
  other arithmetic  4.76 us (2%)
  starting transfers between devices  3.7 us (1%)
  local copies, waits for them, and re-layouts  3.24 us (1%)
    reduce_scatter x1, waiting for transfers between devices, on_device(): lax.psum_scatter(partial_rows, 'col', scatter_dimension=1, tiled=True)  144 us
    all_gather x1, waiting for transfers between devices, on_device(): lax.all_gather(vectors, 'row', axis=1, tiled=True)  58.2 us
    all_to_all x1, waiting for transfers between devices, on_device(): lax.all_to_all(buffer, 'row', split_axis=0, concat_axis=0, tiled=True)  26.4 us
    dot_general x1, matrix products, on_device(): jnp.einsum('ikbr,ikrv->ibv', left_factors, coeffs, preferred_element_type...  17 us
  transfers between devices with their start and end apart: 3, of which 3 were waited for; matrix products, arithmetic and copies ran while one was open for 0% of the time, Pallas kernels for 0%

commit v1 on v0

--- a/solution.py
+++ b/solution.py
@@ -34,14 +34,36 @@
 
 
 def on_device(vectors, right_factors, left_factors, tile_ranks, owner_map):
+
+    def set_the_unit(w_in, in_array):
+        axis_key = "row"
+        clean = lax.psum(1, axis_key)
+        big = lax.axis_index(axis_key)
+        a_next, h_now, x_next = (clean, big, w_in.shape[1])
+        far_arr = range(a_next)
+        next_value = map(lambda hop_no: (hop_no, (hop_no + 1) % a_next), far_arr)
+        even, part_now = (w_in, None)
+        at = 0
+        pieces_in = list(next_value)
+        while at < a_next:
+            before = lax.ppermute(even, axis_key, pieces_in) if at < a_next - 1 else None
+            step_out = in_array(even, (h_now - at) % a_next * x_next)
+            part_now = step_out if part_now is None else part_now + step_out
+            even = before
+            at += 1
+        return part_now
+
     held_rows = right_factors.shape[0]
     rank_width = right_factors.shape[3]
     cycle_size = lax.axis_size("row")
-    products = jnp.einsum(
-        "ikbr,kbv->ikrv",
-        right_factors,
-        lax.all_gather(vectors, "row", axis=1, tiled=True),
-        preferred_element_type=jnp.float32,
+    products = set_the_unit(
+        vectors,
+        lambda own_block, at: jnp.einsum(
+            "ikbr,kbv->ikrv",
+            lax.dynamic_slice_in_dim(right_factors, at, own_block.shape[1], axis=2),
+            own_block,
+            preferred_element_type=jnp.float32,
+        ),
     )
     coeffs = masked_coeffs(products, tile_ranks, rank_width)
     partial_rows = jnp.einsum(

time: 272 us -> 330 us (1.21)
  matrix products: 17 us -> 60.9 us
  waiting for transfers between devices: 229 us -> 243 us
    ppermute x0 -> x7, waiting for transfers between devices: none -> 71.2 us  [set_the_unit(): lax.ppermute(even, axis_key, pieces_in)]
    all_gather x1 -> x0, waiting for transfers between devices: 58.2 us -> none  [on_device(): lax.all_gather(vectors, 'row', axis=1, tiled=True)]
    dot_general x0 -> x7, matrix products: none -> 34.5 us  [on_device(): jnp.einsum('ikbr,kbv->ikrv', lax.dynamic_slice_in_dim(right_factors, at,...]
    dot_general x1, matrix products: 17 us -> 26.4 us  [on_device(): jnp.einsum('ikbr,ikrv->ibv', left_factors, coeffs, preferred_element_type...]
  transfers between devices with their start and end apart: 3 -> 9, of which waited for: 3 -> 9; matrix products, arithmetic and copies ran while one was open for 0% -> 11% of each run, Pallas kernels for 0% -> 0%
where the time goes in v1:
time: 330 us
  waiting for transfers between devices  243 us (74%)
  matrix products  60.9 us (18%)
  between operations  13.5 us (4%)
  other arithmetic  4.89 us (1%)
  starting transfers between devices  4.17 us (1%)
    reduce_scatter x1, waiting for transfers between devices, on_device(): lax.psum_scatter(partial_rows, 'col', scatter_dimension=1, tiled=True)  146 us
    ppermute x7, waiting for transfers between devices, set_the_unit(): lax.ppermute(even, axis_key, pieces_in)  71.2 us
    dot_general x7, matrix products, on_device(): jnp.einsum('ikbr,kbv->ikrv', lax.dynamic_slice_in_dim(right_factors, at,...  34.5 us
    dot_general x1, matrix products, on_device(): jnp.einsum('ikbr,ikrv->ibv', left_factors, coeffs, preferred_element_type...  26.4 us
    all_to_all x1, waiting for transfers between devices, on_device(): lax.all_to_all(buffer, 'row', split_axis=0, concat_axis=0, tiled=True)  26.4 us
  transfers between devices with their start and end apart: 9, of which 9 were waited for; matrix products, arithmetic and copies ran while one was open for 11% of the time, Pallas kernels for 0%

profile of v1, /device:TPU:0, one launch (start us, length us, event | category | flops | bytes accessed | tf_op | source)
XLA Modules:
  0.0 330.1 jit_solution(16218522115521776971)
XLA Ops:
  6.5 0.0 reduce-scatter.2.cloned.1.call-start
  6.5 0.5 collective-permute-start
  7.0 15.6 %collective-permute-done = bf16[8,128,512]{2,1,0:T(8,128)(2,1)S(1)} collective-permute-done((bf16[8,128,512]{2,1,0:T(8,128)(2,1)}, bf16[8,128,512]{2,1,0:T(8,128)(2,1)S(1)}, u32[]{:S(2)}, u32[]{:S(2)}) %collective-permute-start) | collective-permute-done | bytes 1048608 | tf_op jit(solution)/shard_map/ppermute | solution.py:49
  22.6 0.0 collective-permute-start.1
  22.6 15.1 %collective-permute-done.1 = bf16[8,128,512]{2,1,0:T(8,128)(2,1)S(1)} collective-permute-done((bf16[8,128,512]{2,1,0:T(8,128)(2,1)S(1)}, bf16[8,128,512]{2,1,0:T(8,128)(2,1)S(1)}, u32[]{:S(2)}, u32[]{:S(2)}) %collective-permute-start.1) | collective-permute-done | bytes 1048608 | tf_op jit(solution)/shard_map/ppermute | solution.py:49
  37.7 0.0 collective-permute-start.2
  37.7 15.1 %collective-permute-done.2 = bf16[8,128,512]{2,1,0:T(8,128)(2,1)S(1)} collective-permute-done((bf16[8,128,512]{2,1,0:T(8,128)(2,1)S(1)}, bf16[8,128,512]{2,1,0:T(8,128)(2,1)S(1)}, u32[]{:S(2)}, u32[]{:S(2)}) %collective-permute-start.2) | collective-permute-done | bytes 1048608 | tf_op jit(solution)/shard_map/ppermute | solution.py:49
  52.8 0.0 copy-start.1
  52.8 0.0 collective-permute-start.3
  52.8 15.1 %collective-permute-done.3 = bf16[8,128,512]{2,1,0:T(8,128)(2,1)S(1)} collective-permute-done((bf16[8,128,512]{2,1,0:T(8,128)(2,1)S(1)}, bf16[8,128,512]{2,1,0:T(8,128)(2,1)S(1)}, u32[]{:S(2)}, u32[]{:S(2)}) %collective-permute-start.3) | collective-permute-done | bytes 1048608 | tf_op jit(solution)/shard_map/ppermute | solution.py:49
  68.0 0.0 copy-done.1
  68.0 0.0 collective-permute-start.4
  68.0 0.0 copy-start
  68.0 0.9 iota_compare_fusion
  68.9 6.2 %fusion.24 = f32[8,4,128,512]{2,3,0,1:T(8,128)} fusion(bf16[8,128,512]{2,1,0:T(8,128)(2,1)} %param.5, bf16[4,8,1024,128]{3,2,1,0:T(8,128)(2,1)} %param.6, s32[]{:T(128)S(6)} %select_n.144), kind=kOutput, calls=%fused_computation.23 | convolution fusion | flops 536870912 | bytes 10485764 | tf_op jit(solution)/shard_map/ikbr,kbv->ikrv/dot_general | solution.py:61
  75.1 8.1 %collective-permute-done.4 = bf16[8,128,512]{2,1,0:T(8,128)(2,1)} collective-permute-done((bf16[8,128,512]{2,1,0:T(8,128)(2,1)S(1)}, bf16[8,128,512]{2,1,0:T(8,128)(2,1)}, u32[]{:S(2)}, u32[]{:S(2)}) %collective-permute-start.4) | collective-permute-done | bytes 1048608 | tf_op jit(solution)/shard_map/ppermute | solution.py:49
  83.2 0.0 collective-permute-start.5
  83.2 0.0 copy-done
  83.2 4.5 %fusion.22 = f32[8,4,128,512]{2,3,0,1:T(8,128)} fusion(bf16[8,128,512]{2,1,0:T(8,128)(2,1)S(1)} %collective-permute-done, bf16[4,8,1024,128]{3,2,1,0:T(8,128)(2,1)S(1)} %copy-done, s32[]{:T(128)S(6)} %select_n.146), kind=kOutput, calls=%fused_computation.21 | convolution fusion | flops 536870912 | bytes 10485764 | tf_op jit(solution)/shard_map/ikbr,kbv->ikrv/dot_general | solution.py:61
  87.7 0.0 copy-start.2
  87.7 4.5 %fusion.20 = f32[8,4,128,512]{2,3,0,1:T(8,128)} fusion(bf16[8,128,512]{2,1,0:T(8,128)(2,1)S(1)} %collective-permute-done.1, bf16[4,8,1024,128]{3,2,1,0:T(8,128)(2,1)S(1)} %copy-done, s32[]{:T(128)S(6)} %select_n.148), kind=kOutput, calls=%fused_computation.19 | convolution fusion | flops 536870912 | bytes 10485764 | tf_op jit(solution)/shard_map/ikbr,kbv->ikrv/dot_general | solution.py:61
  92.2 0.0 copy-done.2
  92.2 4.5 %fusion.18 = f32[8,4,128,512]{2,3,0,1:T(8,128)} fusion(bf16[8,128,512]{2,1,0:T(8,128)(2,1)S(1)} %copy-done.2, bf16[4,8,1024,128]{3,2,1,0:T(8,128)(2,1)S(1)} %copy-done, s32[]{:T(128)S(6)} %select_n.150), kind=kOutput, calls=%fused_computation.17 | convolution fusion | flops 536870912 | bytes 10485764 | tf_op jit(solution)/shard_map/ikbr,kbv->ikrv/dot_general | solution.py:61
  96.7 1.8 collective-permute-done.5
  98.5 0.0 collective-permute-start.6
  98.5 4.5 %fusion.16 = f32[8,4,128,512]{2,3,0,1:T(8,128)} fusion(bf16[8,128,512]{2,1,0:T(8,128)(2,1)S(1)} %collective-permute-done.3, bf16[4,8,1024,128]{3,2,1,0:T(8,128)(2,1)S(1)} %copy-done, s32[]{:T(128)S(6)} %select_n.152), kind=kOutput, calls=%fused_computation.15 | convolution fusion | flops 536870912 | bytes 10485764 | tf_op jit(solution)/shard_map/ikbr,kbv->ikrv/dot_general | solution.py:61
  103.0 5.7 %fusion.14 = f32[8,4,128,512]{2,3,0,1:T(8,128)} fusion(bf16[8,128,512]{2,1,0:T(8,128)(2,1)} %collective-permute-done.4, bf16[4,8,1024,128]{3,2,1,0:T(8,128)(2,1)S(1)} %copy-done, s32[]{:T(128)S(6)} %select_n.154), kind=kOutput, calls=%fused_computation.13 | convolution fusion | flops 536870912 | bytes 10485764 | tf_op jit(solution)/shard_map/ikbr,kbv->ikrv/dot_general | solution.py:61
  108.8 4.5 %fusion.12 = f32[8,4,128,512]{2,3,0,1:T(8,128)} fusion(bf16[8,128,512]{2,1,0:T(8,128)(2,1)S(1)} %collective-permute-done.5, bf16[4,8,1024,128]{3,2,1,0:T(8,128)(2,1)S(1)} %copy-done, s32[]{:T(128)S(6)} %select_n.156), kind=kOutput, calls=%fused_computation.11 | convolution fusion | flops 536870912 | bytes 10485764 | tf_op jit(solution)/shard_map/ikbr,kbv->ikrv/dot_general | solution.py:61
  113.3 0.4 collective-permute-done.6
  113.7 26.4 %fusion.5 = f32[4,1024,512]{1,2,0:T(8,128)} fusion(bf16[4,8,1024,128]{3,2,1,0:T(8,128)(2,1)} %param.7, f32[8,4,128,512]{2,3,0,1:T(8,128)} %fusion.12, f32[8,4,128,512]{2,3,0,1:T(8,128)} %fusion.14, f32[8,4,128,512]{2,3,0,1:T(8,128)} %fusion.16, f32[8,4,128,512]{2,3,0,1:T(8,128)} %fusion.18, f32[8,4,128,512]{2,3,0,1:T(8,128)} %fusion.20, ...), kind=kOutput, calls=%fused_computation.7 | convolution fusion | flops 4850712576 | bytes 77598720 | tf_op jit(solution)/shard_map/ikbr,ikrv->ibv/dot_general | solution.py:69
  140.1 0.0 copy-start.3
  140.1 0.0 reduce-scatter.2.cloned.1.call-update
  140.1 0.6 copy-done.3
  140.7 0.1 and_select_fusion.1
  140.8 0.1 select_reduce_fusion
  140.9 0.1 fusion.35
  141.0 145.8 %reduce-scatter.2.cloned.1.call-done = f32[4,256,512]{1,2,0:T(8,128)} async-done(((f32[4,1024,512]{1,2,0:T(8,128)}), f32[4,256,512]{1,2,0:T(8,128)}) %reduce-scatter.2.cloned.1.call-update) | async-done | bytes 2097168 | tf_op jit(solution)/shard_map/reduce_scatter | solution.py:72
  286.9 1.7 convert_element_type.7
  288.5 0.7 gather_fusion
  289.2 1.6 select_select_fusion
  290.9 3.7 %all-to-all-start = ((bf16[8,256,512]{1,2,0:T(8,128)(2,1)}), bf16[8,256,512]{1,2,0:T(8,128)(2,1)S(1)}, u32[]{:S(2)}, u32[]{:S(2)}) async-start(bf16[8,256,512]{1,2,0:T(8,128)(2,1)} %select_select_fusion), calls=%async_computation.1 | async-start | bytes 4194304 | tf_op jit(solution)/shard_map/all_to_all | solution.py:76
  294.5 0.2 select_reduce_fusion.1
  294.8 26.4 %all-to-all-done = bf16[8,256,512]{1,2,0:T(8,128)(2,1)S(1)} async-done(((bf16[8,256,512]{1,2,0:T(8,128)(2,1)}), bf16[8,256,512]{1,2,0:T(8,128)(2,1)S(1)}, u32[]{:S(2)}, u32[]{:S(2)}) %all-to-all-start) | async-done | bytes 2097184 | tf_op jit(solution)/shard_map/all_to_all | solution.py:76
  321.1 0.6 gather_fusion.1
  321.8 0.2 broadcast_select_fusion
  321.9 1.3 copy.7
  (7 shorter events, 0.1 us)
Async XLA Ops:
  6.5 280.3 %reduce-scatter.2.cloned.1.call-start = ((), (), s32[]{:S(2)}) async-start(), calls=%async_computation.2 | async-start | bytes 10485760 | tf_op jit(solution)/shard_map/reduce_scatter | solution.py:72
  6.5 16.1 %collective-permute-start = (bf16[8,128,512]{2,1,0:T(8,128)(2,1)}, bf16[8,128,512]{2,1,0:T(8,128)(2,1)S(1)}, u32[]{:S(2)}, u32[]{:S(2)}) collective-permute-start(bf16[8,128,512]{2,1,0:T(8,128)(2,1)} %param.5), channel_id=1, source_target_pairs={{0,4},{4,8},{8,12},{12,16},{16,20},{20,24},{24,28},{28,0},{1,5},{5... | collective-permute-start | bytes 3145736 | tf_op jit(solution)/shard_map/ppermute | solution.py:49
  22.6 15.1 %collective-permute-start.1 = (bf16[8,128,512]{2,1,0:T(8,128)(2,1)S(1)}, bf16[8,128,512]{2,1,0:T(8,128)(2,1)S(1)}, u32[]{:S(2)}, u32[]{:S(2)}) collective-permute-start(bf16[8,128,512]{2,1,0:T(8,128)(2,1)S(1)} %collective-permute-done), channel_id=1, source_target_pairs={{0,4},{4,8},{8,12},{12,16},{16,20},{20,24},{24,28},{28,0},{1,5},{5... | collective-permute-start | bytes 3145736 | tf_op jit(solution)/shard_map/ppermute | solution.py:49
  37.7 15.1 %collective-permute-start.2 = (bf16[8,128,512]{2,1,0:T(8,128)(2,1)S(1)}, bf16[8,128,512]{2,1,0:T(8,128)(2,1)S(1)}, u32[]{:S(2)}, u32[]{:S(2)}) collective-permute-start(bf16[8,128,512]{2,1,0:T(8,128)(2,1)S(1)} %collective-permute-done.1), channel_id=1, source_target_pairs={{0,4},{4,8},{8,12},{12,16},{16,20},{20,24},{24,28},{28,0},{1,5},{5... | collective-permute-start | bytes 3145736 | tf_op jit(solution)/shard_map/ppermute | solution.py:49
  52.8 15.1 %copy-start.1 = (bf16[8,128,512]{2,1,0:T(8,128)(2,1)}, bf16[8,128,512]{2,1,0:T(8,128)(2,1)S(1)}, u32[]{:S(2)}) copy-start(bf16[8,128,512]{2,1,0:T(8,128)(2,1)S(1)} %collective-permute-done.2) | copy-start | bytes 3145732
  52.8 15.1 %collective-permute-start.3 = (bf16[8,128,512]{2,1,0:T(8,128)(2,1)S(1)}, bf16[8,128,512]{2,1,0:T(8,128)(2,1)S(1)}, u32[]{:S(2)}, u32[]{:S(2)}) collective-permute-start(bf16[8,128,512]{2,1,0:T(8,128)(2,1)S(1)} %collective-permute-done.2), channel_id=1, source_target_pairs={{0,4},{4,8},{8,12},{12,16},{16,20},{20,24},{24,28},{28,0},{1,5},{5... | collective-permute-start | bytes 3145736 | tf_op jit(solution)/shard_map/ppermute | solution.py:49
  68.0 15.2 %collective-permute-start.4 = (bf16[8,128,512]{2,1,0:T(8,128)(2,1)S(1)}, bf16[8,128,512]{2,1,0:T(8,128)(2,1)}, u32[]{:S(2)}, u32[]{:S(2)}) collective-permute-start(bf16[8,128,512]{2,1,0:T(8,128)(2,1)S(1)} %collective-permute-done.3), channel_id=1, source_target_pairs={{0,4},{4,8},{8,12},{12,16},{16,20},{20,24},{24,28},{28,0},{1,5},{5... | collective-permute-start | bytes 3145736 | tf_op jit(solution)/shard_map/ppermute | solution.py:49
  68.0 15.2 %copy-start = (bf16[4,8,1024,128]{3,2,1,0:T(8,128)(2,1)S(1)}, bf16[4,8,1024,128]{3,2,1,0:T(8,128)(2,1)}, u32[]{:S(2)}) copy-start(bf16[4,8,1024,128]{3,2,1,0:T(8,128)(2,1)} %param.6) | copy-start | bytes 25165828
  83.2 15.3 %collective-permute-start.5 = (bf16[8,128,512]{2,1,0:T(8,128)(2,1)}, bf16[8,128,512]{2,1,0:T(8,128)(2,1)S(1)}, u32[]{:S(2)}, u32[]{:S(2)}) collective-permute-start(bf16[8,128,512]{2,1,0:T(8,128)(2,1)} %collective-permute-done.4), channel_id=1, source_target_pairs={{0,4},{4,8},{8,12},{12,16},{16,20},{20,24},{24,28},{28,0},{1,5},{5... | collective-permute-start | bytes 3145736 | tf_op jit(solution)/shard_map/ppermute | solution.py:49
  87.7 4.5 %copy-start.2 = (bf16[8,128,512]{2,1,0:T(8,128)(2,1)S(1)}, bf16[8,128,512]{2,1,0:T(8,128)(2,1)}, u32[]{:S(2)}) copy-start(bf16[8,128,512]{2,1,0:T(8,128)(2,1)} %copy-done.1) | copy-start | bytes 3145732
  98.5 15.1 %collective-permute-start.6 = (bf16[8,128,512]{2,1,0:T(8,128)(2,1)S(1)}, bf16[8,128,512]{2,1,0:T(8,128)(2,1)S(1)}, u32[]{:S(2)}, u32[]{:S(2)}) collective-permute-start(bf16[8,128,512]{2,1,0:T(8,128)(2,1)S(1)} %collective-permute-done.5), channel_id=1, source_target_pairs={{0,4},{4,8},{8,12},{12,16},{16,20},{20,24},{24,28},{28,0},{1,5},{5... | collective-permute-start | bytes 3145736 | tf_op jit(solution)/shard_map/ppermute | solution.py:49
  140.1 0.7 copy-start.3
  290.9 30.3 %all-to-all-start = ((bf16[8,256,512]{1,2,0:T(8,128)(2,1)}), bf16[8,256,512]{1,2,0:T(8,128)(2,1)S(1)}, u32[]{:S(2)}, u32[]{:S(2)}) async-start(bf16[8,256,512]{1,2,0:T(8,128)(2,1)} %select_select_fusion), calls=%async_computation.1 | async-start | bytes 4194304 | tf_op jit(solution)/shard_map/all_to_all | solution.py:76
Sparse Core Ops, SparseCore 0:
  140.2 146.5 reduce-scatter.1
